TPU v7x, 256 devices: a whole 4x4x8 slice. The times are simulated.
256 devices in a mesh: seq: 32 (over x, z), batch: 8 (over y, core).
Axes of the slice: x: 4, y: 4, z: 8, core: 2. Of those that a mesh axis runs over, the one named last changes fastest.
Arguments:
- hidden: bfloat16 [16, 8192, 4096], P('batch', None, 'seq')
- gain: float32 [4096], P('seq'), may hold values from 0.5 to 1.5
- value_weight: float32 [4096], P('seq'), may hold values from -0.09375 to 0.09375
- rewards: float32 [16, 8192], P('batch', 'seq'), may hold values from -1.5 to 1.5
- reward_mask: int32 [16, 8192], P('batch', 'seq'), may hold values 0 or 1
- lengths: int32 [16], P('batch'), may hold values from 2048 to 8192
- horizon: float32 [16], P('batch'), may hold values from 24 to 65536
Outputs:
- advantages: float32 [16, 8192], P(None, ('seq', 'batch'))
- returns: float32 [16, 8192], P(None, ('seq', 'batch'))
All inputs are finite; a program needn't handle non-finite values. No bound on the sum of `reward_mask` on one device may be relied on, other than what follows from the above.
Results may differ from a plain program's by a relative error of at most 0.0003.
Values may be sent and summed in bfloat16 or wider, within the bound.
A program may use at most 64 MiB of HBM per device.

v0:
```python
import jax
import jax.numpy as jnp
from jax import lax
from jax.sharding import Mesh
from jax.sharding import PartitionSpec as P

D = 4096
SEQ = ("seq_0", "seq_1")
SEQ_BATCH = ("seq_0", "seq_1", "batch_0", "batch_1")
BATCH = ("batch_0", "batch_1")
EPS = 1e-05


def cut_along(array, dim, devices):
    dims = array.shape
    blocks = array.reshape(*dims[:dim], devices, dims[dim] // devices, *dims[dim + 1 :])
    return jnp.moveaxis(blocks, dim, 0)


def sent_and_summed(array, axis, dim):
    devices = lax.axis_size(axis)
    blocks = lax.all_to_all(cut_along(array, dim, devices), axis, 0, 0, tiled=True)
    return jnp.sum(blocks, axis=0)


def side_by_side(arrays, axis, dim, along):
    widths = [a.shape[along] for a in arrays]
    both = jnp.concatenate(arrays, axis=along)
    whole = sent_and_summed(both, axis, dim)
    return tuple(jnp.split(whole, [sum(widths[:k]) for k in range(1, len(widths))], axis=along))


def from_behind(value, axis, steps):
    count = lax.axis_size(axis)
    initial, last = (max(0, -steps), min(count, count - steps))
    return lax.ppermute(value, axis, [(source, source + steps) for source in range(initial, last)])


def sent_to_all(array, axis):
    devices = lax.axis_size(axis)
    return lax.all_to_all(
        jnp.broadcast_to(array[None], (devices, *array.shape)), axis, 0, 0, tiled=True
    )


def gathered_once(array, axis):
    leaves = jax.tree.leaves(array)
    turns = sorted(range(len(leaves)), key=lambda k: -leaves[k].size)
    width = (1, *leaves[turns[0]].shape)[-1]
    lines = [
        jnp.pad(leaves[k].reshape(-1), (0, -leaves[k].size % width)).reshape(-1, width)
        for k in turns
    ]
    both, at, found = (sent_to_all(jnp.concatenate(lines), axis), 0, {})
    for k, line in zip(turns, lines):
        slab = both[:, at : at + len(line)].reshape(len(both), -1)
        found[k] = slab[:, : leaves[k].size].reshape(-1, *leaves[k].shape)
        at += len(line)
    numbers = iter(range(len(leaves)))
    return jax.tree.map(lambda _: found[next(numbers)], array)


def joined_by_halves(pieces, combine):
    while len(jax.tree.leaves(pieces)[0]) > 1:
        pieces = jax.vmap(combine)(
            *(jax.tree.map(lambda part: part[side::2], pieces) for side in (0, 1))
        )
    return jax.tree.map(lambda part: part[0], pieces)


def prefix(array, axis, combine, identity):
    devices, position = (lax.axis_size(axis), lax.axis_index(axis))
    passed = jnp.arange(devices) > position

    def kept(part, zero, own):
        part = jnp.where(
            passed.reshape(-1, *(1 for _ in own.shape)), part, jnp.asarray(zero, own.dtype)
        )
        return part[::-1]

    pieces = gathered_once(array, axis)
    return joined_by_halves(jax.tree.map(kept, pieces, identity, array), combine)


def one_axis_at_a_time(array, axes):
    for axis in axes:
        array = lax.psum(array, axis)
    return array


def per_device(hidden, gain, value_weight, rewards, reward_mask, lengths, horizon):
    my_index = lax.axis_index(SEQ)
    block = rewards.shape[1]
    wide_rows = hidden.astype(jnp.float32)
    part_squares = jnp.sum(wide_rows * wide_rows, -1)
    part_projected = jnp.sum(wide_rows * (gain * value_weight), -1)
    squares, projected = side_by_side((part_squares, part_projected), SEQ, 1, 0)
    values = projected * lax.rsqrt(squares / D + EPS)
    positions = my_index * block + jnp.arange(block, dtype=jnp.int32)
    valid = (positions[None, :] < lengths[:, None]).astype(jnp.float32)
    next_valid = (positions[None, :] + 1 < lengths[:, None]).astype(jnp.float32)
    following = from_behind(values[:, 0], SEQ, -1)
    next_values = jnp.concatenate([values[:, 1:], following[:, None]], 1)
    delta = (rewards * reward_mask.astype(jnp.float32) + next_valid * next_values - values) * valid
    log_decay = -1.0 / horizon
    offsets = jnp.arange(block, dtype=jnp.int32)
    distance = (offsets[None, :] - offsets[:, None]).astype(jnp.float32)
    upper_mask = distance >= 0.0
    powers = jnp.where(
        upper_mask[None], jnp.exp(jnp.maximum(distance, 0.0)[None] * log_decay[:, None, None]), 0.0
    )
    local_gae = jnp.einsum("rtk,rk->rt", powers, delta, precision=lax.Precision.HIGHEST)
    tail_decay = jnp.exp((block - offsets).astype(jnp.float32)[None, :] * log_decay[:, None])
    start_value = local_gae[:, 0]
    block_decay = jnp.exp(block * log_decay)

    def compose(earlier, later):
        return (later[0] + later[1] * earlier[0], later[1] * earlier[1])

    carry_in, _ = prefix(
        (start_value, block_decay),
        SEQ,
        compose,
        (jnp.zeros_like(start_value), jnp.ones_like(block_decay)),
    )
    gae = local_gae + tail_decay * carry_in[:, None]
    returns = (gae + values) * valid
    count, first, second = (
        one_axis_at_a_time(jnp.sum(valid), SEQ_BATCH),
        one_axis_at_a_time(jnp.sum(gae), SEQ_BATCH),
        one_axis_at_a_time(jnp.sum(gae * gae), SEQ_BATCH),
    )
    mean = first / count
    var = jnp.maximum(second / count - mean * mean, 1.0)
    whitened = (gae - mean) * valid * lax.rsqrt(var)
    out_adv, out_returns = (
        lax.all_to_all(whitened, BATCH, split_axis=1, concat_axis=0, tiled=True),
        lax.all_to_all(returns, BATCH, split_axis=1, concat_axis=0, tiled=True),
    )
    return (out_adv, out_returns)


def solution(mesh):
    finer = Mesh(mesh.devices.reshape(4, 8, 4, 2), ("seq_0", "seq_1", "batch_0", "batch_1"))
    placed = (P(BATCH, None, SEQ), P(SEQ), P(SEQ), P(BATCH, SEQ), P(BATCH, SEQ), P(BATCH), P(BATCH))
    return jax.shard_map(
        per_device,
        mesh=finer,
        in_specs=placed,
        out_specs=(P(None, SEQ_BATCH), P(None, SEQ_BATCH)),
        check_vma=False,
    )
```

profile of v0, /device:TPU:1, one launch (start us, length us, event | category | flops | bytes accessed | tf_op | source)
XLA Modules:
  0.0 118.5 jit_solution(17248735630217335933)
XLA Ops:
  0.6 0.0 copy-start.3
  0.6 0.0 copy-start.1
  0.7 0.0 copy-start.2
  0.7 0.0 copy-start
  0.7 0.7 mul.124
  1.4 6.7 %fusion = (f32[2,8192]{1,0:T(2,128)S(1)}, f32[2,8192]{1,0:T(2,128)S(1)}) fusion(bf16[2,8192,128]{2,1,0:T(8,128)(2,1)} %param.7, f32[128]{0:T(128)S(1)} %mul.124), kind=kLoop, calls=%fused_computation.2 | loop fusion | flops 10452992 | bytes 4325888 | tf_op jit(solution)/shard_map/reduce_sum | solution.py:95
  8.0 0.7 pad_maximum_fusion
  8.7 11.9 %all-to-all-start = ((f32[32,4,256]{2,1,0:T(4,128)}), f32[32,4,256]{2,1,0:T(4,128)S(1)}, u32[]{:S(2)}, u32[]{:S(2)}) async-start(f32[32,4,256]{2,1,0:T(4,128)} %bitcast.1), calls=%async_computation | async-start | bytes 262144 | tf_op jit(solution)/shard_map/all_to_all | solution.py:22
  20.6 0.1 convert_compare_fusion
  20.7 0.0 copy-done.3
  20.8 9.0 %all-to-all-done = f32[32,4,256]{2,1,0:T(4,128)S(1)} async-done(((f32[32,4,256]{2,1,0:T(4,128)}), f32[32,4,256]{2,1,0:T(4,128)S(1)}, u32[]{:S(2)}, u32[]{:S(2)}) %all-to-all-start) | async-done | bytes 131104 | tf_op jit(solution)/shard_map/all_to_all | solution.py:22
  29.8 0.1 slice_reduce_fusion.1
  29.9 0.1 slice.115
  30.0 1.3 %collective-permute-start = (f32[2]{0:T(128)S(1)}, f32[2]{0:T(128)S(1)}, u32[]{:S(2)}, u32[]{:S(2)}) collective-permute-start(f32[2]{0:T(128)S(1)} %slice_reduce_fusion.1), channel_id=1, source_target_pairs={{8,0},{16,8},{24,16},{32,24},{40,32},{48,40},{56,48},{64,56},{72,6... | collective-permute-start | bytes 32 | tf_op jit(solution)/shard_map/ppermute | solution.py:36
  31.3 3.0 %collective-permute-done = f32[2]{0:T(128)S(1)} collective-permute-done((f32[2]{0:T(128)S(1)}, f32[2]{0:T(128)S(1)}, u32[]{:S(2)}, u32[]{:S(2)}) %collective-permute-start) | collective-permute-done | bytes 40 | tf_op jit(solution)/shard_map/ppermute | solution.py:36
  34.3 0.1 copy.15
  34.4 0.0 copy-done.1
  34.4 0.0 copy-done.2
  34.4 0.1 fusion.18
  34.5 0.7 fusion.2
  35.2 0.1 slice_reduce_fusion
  35.3 0.6 broadcast_in_dim.55
  35.9 5.2 %all-to-all-start.1 = ((f32[32,2,2]{2,1,0:T(2,128)}), f32[32,2,2]{2,1,0:T(2,128)S(1)}, u32[]{:S(2)}, u32[]{:S(2)}) async-start(f32[32,2,2]{2,1,0:T(2,128)} %broadcast_in_dim.55), calls=%async_computation.1 | async-start | bytes 65536 | tf_op jit(solution)/shard_map/all_to_all | solution.py:41
  41.1 8.8 %all-to-all-done.1 = f32[32,2,2]{2,1,0:T(2,128)S(1)} async-done(((f32[32,2,2]{2,1,0:T(2,128)}), f32[32,2,2]{2,1,0:T(2,128)S(1)}, u32[]{:S(2)}, u32[]{:S(2)}) %all-to-all-start.1) | async-done | bytes 544 | tf_op jit(solution)/shard_map/all_to_all | solution.py:41
  49.9 0.1 copy.16
  50.0 0.1 copy.17
  50.1 0.1 slice.99
  50.2 0.1 slice.94
  50.3 0.1 slice.91
  50.4 0.1 slice.96
  50.5 0.1 slice.100
  50.6 0.1 slice.92
  50.7 0.1 slice.95
  50.8 0.1 slice.97
  50.9 0.1 slice.101
  51.0 0.1 slice.104
  51.1 0.1 slice.102
  51.2 0.1 slice.98
  51.3 0.1 slice.103
  51.4 0.1 slice.106
  51.5 0.1 slice.105
  51.6 0.1 slice.108
  51.7 0.1 slice.107
  51.8 0.1 slice.110
  51.9 0.1 slice.109
  52.0 0.1 slice.112
  52.1 0.2 add_reduce_fusion
  52.3 0.7 compare_select_fusion
  53.0 0.6 fusion.20
  53.6 7.6 %all-reduce.2 = (f32[]{:T(128)}, f32[]{:T(128)}, f32[]{:T(128)}) all-reduce(f32[]{:T(128)} %get-tuple-element.5, f32[]{:T(128)} %get-tuple-element.24, f32[]{:T(128)} %get-tuple-element.4), channel_id=1, replica_groups=mesh['seq_0'=4,'seq_1'=8,'batch_0'=4,'batch_1'=2] {'seq_0'}, use_global_device_ids=true, to_apply=%region_14.15 | all-reduce | flops 3 | bytes 24 | tf_op jit(solution)/shard_map/psum | solution.py:87
  61.1 11.8 %all-reduce = (f32[]{:T(128)}, f32[]{:T(128)}, f32[]{:T(128)}) all-reduce(f32[]{:T(128)} %get-tuple-element.12, f32[]{:T(128)} %get-tuple-element.13, f32[]{:T(128)} %get-tuple-element.14), channel_id=1, replica_groups=mesh['seq_0'=4,'seq_1'=8,'batch_0'=4,'batch_1'=2] {'seq_1'}, use_global_device_ids=true, to_apply=%region_15.16 | all-reduce | flops 3 | bytes 24 | tf_op jit(solution)/shard_map/psum | solution.py:87
  72.9 9.7 %all-reduce.1 = (f32[]{:T(128)}, f32[]{:T(128)}, f32[]{:T(128)}) all-reduce(f32[]{:T(128)} %get-tuple-element.6, f32[]{:T(128)} %get-tuple-element.7, f32[]{:T(128)} %get-tuple-element.8), channel_id=1, replica_groups=mesh['seq_0'=4,'seq_1'=8,'batch_0'=4,'batch_1'=2] {'batch_0'}, use_global_device_ids=true, to_apply=%region_16.17 | all-reduce | flops 3 | bytes 24 | tf_op jit(solution)/shard_map/psum | solution.py:87
  82.6 14.5 %all-reduce.3 = (f32[]{:T(128)}, f32[]{:T(128)}, f32[]{:T(128)}) all-reduce(f32[]{:T(128)} %get-tuple-element.9, f32[]{:T(128)} %get-tuple-element.10, f32[]{:T(128)} %get-tuple-element.11), channel_id=1, replica_groups=mesh['seq_0'=4,'seq_1'=8,'batch_0'=4,'batch_1'=2] {'batch_1'}, use_global_device_ids=true, to_apply=%region_17.18 | all-reduce | flops 3 | bytes 24 | tf_op jit(solution)/shard_map/psum | solution.py:87
  99.8 0.1 fusion.13
  99.9 0.1 all_to_all.36
  99.9 0.6 copy.18
  100.6 3.6 %all-to-all-start.2 = ((f32[2,8,32]{2,0,1:T(2,128)}), f32[2,8,32]{2,0,1:T(2,128)S(1)}, u32[]{:S(2)}, u32[]{:S(2)}) async-start(f32[2,8,32]{2,0,1:T(2,128)} %copy.18), calls=%async_computation.2 | async-start | bytes 16384 | tf_op jit(solution)/shard_map/all_to_all | solution.py:137
  104.1 0.1 all_to_all.40
  104.2 0.6 copy.19
  104.8 4.0 %all-to-all-done.2 = f32[2,8,32]{2,0,1:T(2,128)S(1)} async-done(((f32[2,8,32]{2,0,1:T(2,128)}), f32[2,8,32]{2,0,1:T(2,128)S(1)}, u32[]{:S(2)}, u32[]{:S(2)}) %all-to-all-start.2) | async-done | bytes 2080 | tf_op jit(solution)/shard_map/all_to_all | solution.py:137
  108.8 3.9 %all-to-all-start.3 = ((f32[2,8,32]{2,0,1:T(2,128)}), f32[2,8,32]{2,0,1:T(2,128)S(1)}, u32[]{:S(2)}, u32[]{:S(2)}) async-start(f32[2,8,32]{2,0,1:T(2,128)} %copy.19), calls=%async_computation.3 | async-start | bytes 16384 | tf_op jit(solution)/shard_map/all_to_all | solution.py:138
  112.7 4.6 %all-to-all-done.3 = f32[2,8,32]{2,0,1:T(2,128)S(1)} async-done(((f32[2,8,32]{2,0,1:T(2,128)}), f32[2,8,32]{2,0,1:T(2,128)S(1)}, u32[]{:S(2)}, u32[]{:S(2)}) %all-to-all-start.3) | async-done | bytes 2080 | tf_op jit(solution)/shard_map/all_to_all | solution.py:138
  117.4 0.6 copy.31
  118.0 0.6 copy.32
  (16 shorter events, 0.2 us)
Async XLA Ops:
  0.6 20.1 %copy-start.3 = (f32[2]{0:T(128)S(1)}, f32[2]{0:T(128)}, u32[]{:S(2)}) copy-start(f32[2]{0:T(128)} %param.13) | copy-start | bytes 28
  0.6 33.8 %copy-start.1 = (f32[2,256]{1,0:T(2,128)S(1)}, f32[2,256]{1,0:T(2,128)}, u32[]{:S(2)}) copy-start(f32[2,256]{1,0:T(2,128)} %param.10) | copy-start | bytes 6148
  0.7 33.7 %copy-start.2 = (s32[2,256]{1,0:T(2,128)S(1)}, s32[2,256]{1,0:T(2,128)}, u32[]{:S(2)}) copy-start(s32[2,256]{1,0:T(2,128)} %param.11) | copy-start | bytes 6148
  0.7 33.7 %copy-start = (s32[2]{0:T(128)S(1)}, s32[2]{0:T(128)}, u32[]{:S(2)}) copy-start(s32[2]{0:T(128)} %param.12) | copy-start | bytes 28
  8.7 21.0 %all-to-all-start = ((f32[32,4,256]{2,1,0:T(4,128)}), f32[32,4,256]{2,1,0:T(4,128)S(1)}, u32[]{:S(2)}, u32[]{:S(2)}) async-start(f32[32,4,256]{2,1,0:T(4,128)} %bitcast.1), calls=%async_computation | async-start | bytes 262144 | tf_op jit(solution)/shard_map/all_to_all | solution.py:22
  30.0 4.3 %collective-permute-start = (f32[2]{0:T(128)S(1)}, f32[2]{0:T(128)S(1)}, u32[]{:S(2)}, u32[]{:S(2)}) collective-permute-start(f32[2]{0:T(128)S(1)} %slice_reduce_fusion.1), channel_id=1, source_target_pairs={{8,0},{16,8},{24,16},{32,24},{40,32},{48,40},{56,48},{64,56},{72,6... | collective-permute-start | bytes 32 | tf_op jit(solution)/shard_map/ppermute | solution.py:36
  35.9 13.9 %all-to-all-start.1 = ((f32[32,2,2]{2,1,0:T(2,128)}), f32[32,2,2]{2,1,0:T(2,128)S(1)}, u32[]{:S(2)}, u32[]{:S(2)}) async-start(f32[32,2,2]{2,1,0:T(2,128)} %broadcast_in_dim.55), calls=%async_computation.1 | async-start | bytes 65536 | tf_op jit(solution)/shard_map/all_to_all | solution.py:41
  100.6 8.2 %all-to-all-start.2 = ((f32[2,8,32]{2,0,1:T(2,128)}), f32[2,8,32]{2,0,1:T(2,128)S(1)}, u32[]{:S(2)}, u32[]{:S(2)}) async-start(f32[2,8,32]{2,0,1:T(2,128)} %copy.18), calls=%async_computation.2 | async-start | bytes 16384 | tf_op jit(solution)/shard_map/all_to_all | solution.py:137
  108.8 8.6 %all-to-all-start.3 = ((f32[2,8,32]{2,0,1:T(2,128)}), f32[2,8,32]{2,0,1:T(2,128)S(1)}, u32[]{:S(2)}, u32[]{:S(2)}) async-start(f32[2,8,32]{2,0,1:T(2,128)} %copy.19), calls=%async_computation.3 | async-start | bytes 16384 | tf_op jit(solution)/shard_map/all_to_all | solution.py:138
where the time goes:
time: 119 us
  blocking collectives  43.6 us (37%)
  waiting for transfers between devices  29.3 us (25%)
  starting transfers between devices  25.8 us (22%)
  other arithmetic  9.9 us (8%)
  local copies, waits for them, and re-layouts  5.74 us (5%)
  between operations  3.44 us (3%)
    psum x4, blocking collectives, one_axis_at_a_time(): array = lax.psum(array, axis)  43.6 us
    all_to_all x1, starting transfers between devices, sent_and_summed(): lax.all_to_all(cut_along(array, dim, devices), axis, 0, 0, tiled=True)  11.9 us
    all_to_all x1, waiting for transfers between devices, sent_and_summed(): lax.all_to_all(cut_along(array, dim, devices), axis, 0, 0, tiled=True)  8.98 us
    all_to_all x1, waiting for transfers between devices, sent_to_all(): lax.all_to_all(jnp.broadcast_to(array[None], (devices, *array.shape)), ax...  8.76 us
    reduce_sum x1, other arithmetic, per_device(): part_squares = jnp.sum(wide_rows * wide_rows, -1)  6.65 us
    all_to_all x1, starting transfers between devices, sent_to_all(): lax.all_to_all(jnp.broadcast_to(array[None], (devices, *array.shape)), ax...  5.16 us
    all_to_all x1, waiting for transfers between devices, per_device(): lax.all_to_all(returns, BATCH, split_axis=1, concat_axis=0, tiled=True)  4.64 us
    all_to_all x1, waiting for transfers between devices, per_device(): lax.all_to_all(whitened, BATCH, split_axis=1, concat_axis=0, tiled=True)  3.96 us
  transfers between devices with their start and end apart: 5, of which 5 were waited for; matrix products, arithmetic and copies ran while one was open for 1% of the time, Pallas kernels for 0%

commit v1 on v0

--- a/solution.py
+++ b/solution.py
@@ -135,7 +135,12 @@
     whitened = (gae - mean) * valid * lax.rsqrt(var)
     out_adv, out_returns = (
         lax.all_to_all(whitened, BATCH, split_axis=1, concat_axis=0, tiled=True),
-        lax.all_to_all(returns, BATCH, split_axis=1, concat_axis=0, tiled=True),
+        jnp.concatenate(
+            lax.all_to_all(
+                jnp.stack(jnp.split(returns, lax.axis_size(BATCH), axis=1)), BATCH, 0, 0
+            ),
+            axis=0,
+        ),
     )
     return (out_adv, out_returns)
 

time: 119 us -> 120 us (level)
  starting transfers between devices: 25.8 us -> 30.7 us
  local copies, waits for them, and re-layouts: 5.74 us -> 9.98 us
  blocking collectives: 43.6 us -> 39.6 us
  waiting for transfers between devices: 29.3 us -> 25.4 us
    all_to_all x1, starting transfers between devices: 3.94 us -> 8.85 us  [per_device(): lax.all_to_all(jnp.stack(jnp.split(returns, lax.axis_size(BATCH), axis=1)...]
    all_to_all x1, waiting for transfers between devices: 4.64 us -> 0.01 us  [per_device(): lax.all_to_all(jnp.stack(jnp.split(returns, lax.axis_size(BATCH), axis=1)...]
    unnamed x10 -> x17, local copies, waits for them, and re-layouts: 1.21 us -> 5.5 us
    psum x4, blocking collectives: 43.6 us -> 39.6 us  [one_axis_at_a_time(): array = lax.psum(array, axis)]
  transfers between devices with their start and end apart: 5 -> 5, of which waited for: 5 -> 4; matrix products, arithmetic and copies ran while one was open for 1% -> 1% of each run, Pallas kernels for 0% -> 0%
where the time goes in v1:
time: 120 us
  blocking collectives  39.6 us (33%)
  starting transfers between devices  30.7 us (26%)
  waiting for transfers between devices  25.4 us (21%)
  local copies, waits for them, and re-layouts  9.98 us (8%)
  other arithmetic  9.97 us (8%)
  between operations  3.5 us (3%)
    psum x4, blocking collectives, one_axis_at_a_time(): array = lax.psum(array, axis)  39.6 us
    all_to_all x1, starting transfers between devices, sent_and_summed(): lax.all_to_all(cut_along(array, dim, devices), axis, 0, 0, tiled=True)  11.9 us
    all_to_all x1, waiting for transfers between devices, sent_and_summed(): lax.all_to_all(cut_along(array, dim, devices), axis, 0, 0, tiled=True)  8.98 us
    all_to_all x1, starting transfers between devices, per_device(): lax.all_to_all(jnp.stack(jnp.split(returns, lax.axis_size(BATCH), axis=1)...  8.85 us
    all_to_all x1, waiting for transfers between devices, sent_to_all(): lax.all_to_all(jnp.broadcast_to(array[None], (devices, *array.shape)), ax...  8.76 us
    reduce_sum x1, other arithmetic, per_device(): part_squares = jnp.sum(wide_rows * wide_rows, -1)  6.65 us
    unnamed x17, local copies, waits for them, and re-layouts  5.5 us
    all_to_all x1, starting transfers between devices, sent_to_all(): lax.all_to_all(jnp.broadcast_to(array[None], (devices, *array.shape)), ax...  5.16 us
  transfers between devices with their start and end apart: 5, of which 4 were waited for; matrix products, arithmetic and copies ran while one was open for 1% of the time, Pallas kernels for 0%

profile of v1, /device:TPU:1, one launch (start us, length us, event | category | flops | bytes accessed | tf_op | source)
XLA Modules:
  0.0 119.8 jit_solution(16517939303517614086)
XLA Ops:
  0.6 0.0 copy-start.3
  0.7 0.7 mul.124
  1.4 6.7 %fusion = (f32[2,8192]{1,0:T(2,128)S(1)}, f32[2,8192]{1,0:T(2,128)S(1)}) fusion(bf16[2,8192,128]{2,1,0:T(8,128)(2,1)} %param.7, f32[128]{0:T(128)S(1)} %mul.124), kind=kLoop, calls=%fused_computation.2 | loop fusion | flops 10452992 | bytes 4325888 | tf_op jit(solution)/shard_map/reduce_sum | solution.py:95
  8.0 0.7 pad_maximum_fusion
  8.7 11.9 %all-to-all-start = ((f32[32,4,256]{2,1,0:T(4,128)}), f32[32,4,256]{2,1,0:T(4,128)S(1)}, u32[]{:S(2)}, u32[]{:S(2)}) async-start(f32[32,4,256]{2,1,0:T(4,128)} %bitcast.1), calls=%async_computation | async-start | bytes 262144 | tf_op jit(solution)/shard_map/all_to_all | solution.py:22
  20.6 0.1 convert_compare_fusion
  20.8 9.0 %all-to-all-done = f32[32,4,256]{2,1,0:T(4,128)S(1)} async-done(((f32[32,4,256]{2,1,0:T(4,128)}), f32[32,4,256]{2,1,0:T(4,128)S(1)}, u32[]{:S(2)}, u32[]{:S(2)}) %all-to-all-start) | async-done | bytes 131104 | tf_op jit(solution)/shard_map/all_to_all | solution.py:22
  29.8 0.1 slice_reduce_fusion.1
  29.9 0.1 slice.115
  30.0 1.3 %collective-permute-start = (f32[2]{0:T(128)S(1)}, f32[2]{0:T(128)S(1)}, u32[]{:S(2)}, u32[]{:S(2)}) collective-permute-start(f32[2]{0:T(128)S(1)} %slice_reduce_fusion.1), channel_id=1, source_target_pairs={{8,0},{16,8},{24,16},{32,24},{40,32},{48,40},{56,48},{64,56},{72,6... | collective-permute-start | bytes 32 | tf_op jit(solution)/shard_map/ppermute | solution.py:36
  31.3 3.0 %collective-permute-done = f32[2]{0:T(128)S(1)} collective-permute-done((f32[2]{0:T(128)S(1)}, f32[2]{0:T(128)S(1)}, u32[]{:S(2)}, u32[]{:S(2)}) %collective-permute-start) | collective-permute-done | bytes 40 | tf_op jit(solution)/shard_map/ppermute | solution.py:36
  34.3 0.1 copy.13
  34.4 0.1 fusion.18
  34.5 0.7 fusion.2
  35.2 0.1 slice_reduce_fusion
  35.3 0.6 broadcast_in_dim.55
  35.9 5.2 %all-to-all-start.1 = ((f32[32,2,2]{2,1,0:T(2,128)}), f32[32,2,2]{2,1,0:T(2,128)S(1)}, u32[]{:S(2)}, u32[]{:S(2)}) async-start(f32[32,2,2]{2,1,0:T(2,128)} %broadcast_in_dim.55), calls=%async_computation.1 | async-start | bytes 65536 | tf_op jit(solution)/shard_map/all_to_all | solution.py:41
  41.1 8.8 %all-to-all-done.1 = f32[32,2,2]{2,1,0:T(2,128)S(1)} async-done(((f32[32,2,2]{2,1,0:T(2,128)}), f32[32,2,2]{2,1,0:T(2,128)S(1)}, u32[]{:S(2)}, u32[]{:S(2)}) %all-to-all-start.1) | async-done | bytes 544 | tf_op jit(solution)/shard_map/all_to_all | solution.py:41
  49.9 0.1 copy.14
  50.0 0.1 copy.15
  50.1 0.1 slice.99
  50.2 0.1 slice.94
  50.3 0.1 slice.91
  50.4 0.1 slice.96
  50.5 0.1 slice.100
  50.6 0.1 slice.92
  50.7 0.1 slice.95
  50.8 0.1 slice.97
  50.9 0.1 slice.101
  51.0 0.1 slice.104
  51.1 0.1 slice.102
  51.2 0.1 slice.98
  51.3 0.1 slice.103
  51.4 0.1 slice.106
  51.5 0.1 slice.105
  51.6 0.1 slice.108
  51.7 0.1 slice.107
  51.8 0.1 slice.110
  51.9 0.1 slice.109
  52.0 0.1 slice.112
  52.1 0.2 add_reduce_fusion
  52.3 0.7 compare_select_fusion
  53.0 0.6 constant_dynamic-update-slice_fusion.7
  53.5 0.6 constant_dynamic-update-slice_fusion.6
  54.2 0.6 constant_dynamic-update-slice_fusion.5
  54.8 0.6 constant_dynamic-update-slice_fusion.4
  55.4 0.6 constant_dynamic-update-slice_fusion.3
  56.0 0.6 constant_dynamic-update-slice_fusion.2
  56.6 0.6 constant_dynamic-update-slice_fusion.1
  57.2 0.6 constant_dynamic-update-slice_fusion
  57.9 8.9 %all-to-all-start.3 = ((f32[8,2,32]{2,1,0:T(2,128)}), f32[8,2,32]{2,1,0:T(2,128)S(1)}, u32[]{:S(2)}, u32[]{:S(2)}) async-start(f32[8,2,32]{2,1,0:T(2,128)} %constant_dynamic-update-slice_fusion), calls=%async_computation.3 | async-start | bytes 16384 | tf_op jit(solution)/shard_map/all_to_all | solution.py:139
  66.7 0.7 fusion.20
  67.4 7.6 %all-reduce.2 = (f32[]{:T(128)}, f32[]{:T(128)}, f32[]{:T(128)}) all-reduce(f32[]{:T(128)} %get-tuple-element.5, f32[]{:T(128)} %get-tuple-element.24, f32[]{:T(128)} %get-tuple-element.4), channel_id=1, replica_groups=mesh['seq_0'=4,'seq_1'=8,'batch_0'=4,'batch_1'=2] {'seq_0'}, use_global_device_ids=true, to_apply=%region_14.15 | all-reduce | flops 3 | bytes 24 | tf_op jit(solution)/shard_map/psum | solution.py:87
  75.0 11.8 %all-reduce = (f32[]{:T(128)}, f32[]{:T(128)}, f32[]{:T(128)}) all-reduce(f32[]{:T(128)} %get-tuple-element.12, f32[]{:T(128)} %get-tuple-element.13, f32[]{:T(128)} %get-tuple-element.14), channel_id=1, replica_groups=mesh['seq_0'=4,'seq_1'=8,'batch_0'=4,'batch_1'=2] {'seq_1'}, use_global_device_ids=true, to_apply=%region_15.16 | all-reduce | flops 3 | bytes 24 | tf_op jit(solution)/shard_map/psum | solution.py:87
  86.7 9.3 %all-reduce.1 = (f32[]{:T(128)}, f32[]{:T(128)}, f32[]{:T(128)}) all-reduce(f32[]{:T(128)} %get-tuple-element.6, f32[]{:T(128)} %get-tuple-element.7, f32[]{:T(128)} %get-tuple-element.8), channel_id=1, replica_groups=mesh['seq_0'=4,'seq_1'=8,'batch_0'=4,'batch_1'=2] {'batch_0'}, use_global_device_ids=true, to_apply=%region_16.17 | all-reduce | flops 3 | bytes 24 | tf_op jit(solution)/shard_map/psum | solution.py:87
  96.1 10.9 %all-reduce.3 = (f32[]{:T(128)}, f32[]{:T(128)}, f32[]{:T(128)}) all-reduce(f32[]{:T(128)} %get-tuple-element.9, f32[]{:T(128)} %get-tuple-element.10, f32[]{:T(128)} %get-tuple-element.11), channel_id=1, replica_groups=mesh['seq_0'=4,'seq_1'=8,'batch_0'=4,'batch_1'=2] {'batch_1'}, use_global_device_ids=true, to_apply=%region_17.18 | all-reduce | flops 3 | bytes 24 | tf_op jit(solution)/shard_map/psum | solution.py:87
  109.7 0.1 fusion.13
  109.7 0.1 all_to_all.25
  109.8 0.6 copy.16
  110.4 0.0 all-to-all-done.3
  110.4 3.6 %all-to-all-start.2 = ((f32[2,8,32]{2,0,1:T(2,128)}), f32[2,8,32]{2,0,1:T(2,128)S(1)}, u32[]{:S(2)}, u32[]{:S(2)}) async-start(f32[2,8,32]{2,0,1:T(2,128)} %copy.16), calls=%async_computation.2 | async-start | bytes 16384 | tf_op jit(solution)/shard_map/all_to_all | solution.py:137
  114.0 4.6 %all-to-all-done.2 = f32[2,8,32]{2,0,1:T(2,128)S(1)} async-done(((f32[2,8,32]{2,0,1:T(2,128)}), f32[2,8,32]{2,0,1:T(2,128)S(1)}, u32[]{:S(2)}, u32[]{:S(2)}) %all-to-all-start.2) | async-done | bytes 2080 | tf_op jit(solution)/shard_map/all_to_all | solution.py:137
  118.6 0.6 copy.35
  119.2 0.6 copy.36
  (22 shorter events, 0.2 us)
Async XLA Ops:
  0.6 20.1 %copy-start.3 = (f32[2]{0:T(128)S(1)}, f32[2]{0:T(128)}, u32[]{:S(2)}) copy-start(f32[2]{0:T(128)} %param.13) | copy-start | bytes 28
  0.6 33.8 %copy-start.1 = (f32[2,256]{1,0:T(2,128)S(1)}, f32[2,256]{1,0:T(2,128)}, u32[]{:S(2)}) copy-start(f32[2,256]{1,0:T(2,128)} %param.10) | copy-start | bytes 6148
  0.7 33.7 %copy-start.2 = (s32[2,256]{1,0:T(2,128)S(1)}, s32[2,256]{1,0:T(2,128)}, u32[]{:S(2)}) copy-start(s32[2,256]{1,0:T(2,128)} %param.11) | copy-start | bytes 6148
  0.7 33.7 %copy-start = (s32[2]{0:T(128)S(1)}, s32[2]{0:T(128)}, u32[]{:S(2)}) copy-start(s32[2]{0:T(128)} %param.12) | copy-start | bytes 28
  8.7 21.0 %all-to-all-start = ((f32[32,4,256]{2,1,0:T(4,128)}), f32[32,4,256]{2,1,0:T(4,128)S(1)}, u32[]{:S(2)}, u32[]{:S(2)}) async-start(f32[32,4,256]{2,1,0:T(4,128)} %bitcast.1), calls=%async_computation | async-start | bytes 262144 | tf_op jit(solution)/shard_map/all_to_all | solution.py:22
  30.0 4.3 %collective-permute-start = (f32[2]{0:T(128)S(1)}, f32[2]{0:T(128)S(1)}, u32[]{:S(2)}, u32[]{:S(2)}) collective-permute-start(f32[2]{0:T(128)S(1)} %slice_reduce_fusion.1), channel_id=1, source_target_pairs={{8,0},{16,8},{24,16},{32,24},{40,32},{48,40},{56,48},{64,56},{72,6... | collective-permute-start | bytes 32 | tf_op jit(solution)/shard_map/ppermute | solution.py:36
  35.9 13.9 %all-to-all-start.1 = ((f32[32,2,2]{2,1,0:T(2,128)}), f32[32,2,2]{2,1,0:T(2,128)S(1)}, u32[]{:S(2)}, u32[]{:S(2)}) async-start(f32[32,2,2]{2,1,0:T(2,128)} %broadcast_in_dim.55), calls=%async_computation.1 | async-start | bytes 65536 | tf_op jit(solution)/shard_map/all_to_all | solution.py:41
  57.9 52.5 %all-to-all-start.3 = ((f32[8,2,32]{2,1,0:T(2,128)}), f32[8,2,32]{2,1,0:T(2,128)S(1)}, u32[]{:S(2)}, u32[]{:S(2)}) async-start(f32[8,2,32]{2,1,0:T(2,128)} %constant_dynamic-update-slice_fusion), calls=%async_computation.3 | async-start | bytes 16384 | tf_op jit(solution)/shard_map/all_to_all | solution.py:139
  110.4 8.2 %all-to-all-start.2 = ((f32[2,8,32]{2,0,1:T(2,128)}), f32[2,8,32]{2,0,1:T(2,128)S(1)}, u32[]{:S(2)}, u32[]{:S(2)}) async-start(f32[2,8,32]{2,0,1:T(2,128)} %copy.16), calls=%async_computation.2 | async-start | bytes 16384 | tf_op jit(solution)/shard_map/all_to_all | solution.py:137
